TPU v7x, 256 devices: a whole 4x4x8 slice. The times are simulated.
256 devices in a mesh: gx: 8 (over y_hi, x), gy: 8 (over z), gz: 4 (over y_lo, core).
Axes of the slice: x: 4, y: 4 (y_hi: 2, y_lo: 2; y = y_hi * 2 + y_lo), z: 8, core: 2. Of those that a mesh axis runs over, the one named last changes fastest.
Arguments:
- tokens: bfloat16 [4096, 49, 512], P(('gx', 'gy', 'gz')), may hold values from -6 to 6
- cotangent: bfloat16 [4096, 49, 512], P(('gx', 'gy', 'gz')), may hold values from -6 to 6
- regions: int32 [4096, 49], P(('gx', 'gy', 'gz')), may hold values from 0 to 3
- rel_index: int32 [49, 49], replicated, may hold values from 0 to 168
- w_qkv: bfloat16 [512, 1536], replicated, may hold values from -0.25 to 0.25
- w_proj: bfloat16 [512, 512], replicated, may hold values from -0.25 to 0.25
- bias_table: float32 [169, 16], replicated, may hold values from -4 to 4
- mom_qkv: float32 [786432], P(('gx', 'gy', 'gz')), may hold values from -0.06 to 0.06
- mom_proj: float32 [262144], P(('gx', 'gy', 'gz')), may hold values from -0.06 to 0.06
- mom_table: float32 [169, 16], replicated, may hold values from -0.06 to 0.06
Outputs:
- new_mom_qkv: float32 [786432], P(('gx', 'gy', 'gz'))
- new_mom_proj: float32 [262144], P(('gx', 'gy', 'gz'))
- new_mom_table: float32 [169, 16], replicated
All inputs are finite; a program needn't handle non-finite values.
Results may differ from a plain program's by a relative error of at most 0.015.
Values sent between devices are 32-bit elements; how exact they have to be, the bound alone decides.
No kernel may reach another device: no remote copies, remote signals or barrier semaphores. Data moves between devices by JAX's collectives and lax.ppermute only.
A program may use at most 128 MiB of HBM per device.

v0:
```python
import jax
import jax.numpy as jnp
from jax import lax
from jax.experimental import pallas as pl
from jax.experimental.pallas import tpu as pltpu
from jax.sharding import PartitionSpec as P


AXES = ("gx", "gy", "gz")
WIN = 16
TOK = 49
PAD = 64
D = 512
HEADS = 16
HD = 32
ENT = 169
EPAD = 176
UNROLL = 8
OFFSETS = (2, 1, 3, 0)
AHEAD = 2
ROWS = TOK * WIN
PROWS = PAD * WIN
F32 = jnp.float32
BF16 = jnp.bfloat16
NT = (((1,), (1,)), ((), ()))
NN = (((1,), (0,)), ((), ()))


def dot(a, b, dims=NN):
    return lax.dot_general(a, b, dims, preferred_element_type=F32)


def decode(flat):
    gx, gy, gz = flat // 32, (flat // 4) % 8, flat % 4
    return gx % 4, (gx // 4) * 2 + gz // 2, gy, gz % 2


def encode(x, y, z, c):
    x, y, z = x % 4, y % 4, z % 8
    return ((y // 2) * 4 + x) * 32 + z * 4 + (y % 2) * 2 + c


def shift(value, dx=0, dy=0, dz=0, dc=0):
    pairs = []
    for d in range(256):
        x, y, z, c = decode(d)
        pairs.append((d, encode(x + dx, y + dy, z + dz, c ^ dc)))
    return lax.ppermute(value, AXES, pairs)


def reorder(core, src, dst):
    r = lax.broadcasted_iota(jnp.int32, (128, 128), 0)
    col = lax.broadcasted_iota(jnp.int32, (128, 128), 1)
    e = r & 1
    z = (r >> 1) & 7
    x = (r >> 4) & 3
    y0 = (r >> 6) & 1
    for rc in range(2):
        c = (rc + core) & 1
        orig = ((x * 32 + z * 4 + y0 * 2 + c) << 1) + e
        hot = jnp.concatenate([jnp.where(orig == col + 128 * k, 1.0, 0.0) for k in range(2)], axis=1).astype(BF16)
        for y1 in range(2):
            at = 256 * rc + 128 * y1
            dst[at : at + 128] = dot(hot, src[:, 256 * y1 : 256 * y1 + 256], NT).astype(BF16)


def local_kernel(
    tok_h, cot_h, reg_h, rel_h, wqkv_h, wproj_h, tab_h, keep, send,
    tok, cot, reg, rel, wqkv, wproj, tab, sems, tokw, cotw, qkv_s, da_s, att_s, dqkv_s, bias_s, mask_s, acc_s, sq_s, t_s,
):
    moves = [
        pltpu.make_async_copy(src, dst, sems.at[n])
        for n, (src, dst) in enumerate(
            zip((tok_h, rel_h, reg_h, tab_h, wqkv_h, cot_h, wproj_h), (tok, rel, reg, tab, wqkv, cot, wproj))
        )
    ]
    for move in moves:
        move.start()
    factor = 1.4426950408889634
    scale = HD**-0.5

    line = lax.broadcasted_iota(jnp.int32, (256, 128), 0)
    lanes = lax.broadcasted_iota(jnp.int32, (256, 128), 1)
    source = (line & 15) * WIN + (line >> 4)
    pick = jnp.concatenate([jnp.where(source == lanes + 128 * k, 1.0, 0.0) for k in range(2)], axis=1).astype(BF16)
    alone = jnp.where(((line & 15) == 0) & ((line >> 4) == lanes), 1.0, 0.0).astype(BF16)[:, 0:WIN]

    def regroup(src, dst):
        for b in range(4):
            if b < 3:
                moved = dot(pick, src[256 * b : 256 * b + 256]).astype(BF16)
            else:
                moved = dot(alone, src[768:784]).astype(BF16)
            for w in range(WIN):
                dst[w * PAD + 16 * b : w * PAD + 16 * b + 16] = moved[16 * w : 16 * w + 16]

    for move in moves[0:4]:
        move.wait()
    regroup(tok, tokw)

    sq_s[...] = jnp.zeros((128, 128), F32)
    sq_s[0:TOK, 0:TOK] = rel[...].astype(F32)
    sq_s[PAD : PAD + TOK, 0:TOK] = rel[...].astype(F32)
    relt = jnp.transpose(sq_s[...])[0:PAD].astype(jnp.int32)
    lane = lax.broadcasted_iota(jnp.int32, (PAD, 128), 1)
    sub = lax.broadcasted_iota(jnp.int32, (PAD, 128), 0)
    live = ((lane & 63) < TOK) & (sub < TOK)
    relt = jnp.where(live, relt, -1)
    safe = jnp.where(live, relt, 0)
    low_i = jnp.where(safe < 128, safe, 0)
    high_i = jnp.where(safe < 128, 0, safe - 128)
    is_low = safe < 128
    first = lane < 64
    for hp in range(HEADS // 2):
        looked = []
        for par in range(2):
            h = 2 * hp + par
            low = jnp.broadcast_to(tab[h : h + 1, 0:128], (8, 128))
            high = jnp.concatenate([tab[h : h + 1, 128:ENT], jnp.zeros((1, 256 - ENT), F32)], axis=1)
            high = jnp.broadcast_to(high, (8, 128))
            rows = []
            for b in range(PAD // 8):
                s = slice(8 * b, 8 * b + 8)
                a0 = jnp.take_along_axis(low, low_i[s], axis=1, mode="promise_in_bounds")
                a1 = jnp.take_along_axis(high, high_i[s], axis=1, mode="promise_in_bounds")
                rows.append(jnp.where(is_low[s], a0, a1))
            looked.append(jnp.concatenate(rows, axis=0))
        both = jnp.where(first, looked[0], looked[1])
        bias_s[hp * PAD : (hp + 1) * PAD] = jnp.where(sub < TOK, both * factor, -1e30)

    sq_s[...] = jnp.zeros((128, 128), F32)
    sq_s[0:WIN, 0:TOK] = reg[...].astype(F32)
    base = sq_s[...]
    cols = jnp.transpose(base)
    for w in range(WIN):
        row = jnp.concatenate([base[w : w + 1, 0:64], base[w : w + 1, 0:64]], axis=1)
        mask_s[w * PAD : (w + 1) * PAD] = jnp.where(cols[0:PAD, w : w + 1] == row, 0.0, -100.0 * factor)

    acc_s[...] = jnp.zeros(acc_s.shape, F32)

    for move in moves[4:7]:
        move.wait()
    regroup(cot, cotw)
    for n in range(6):
        cols = slice(256 * n, 256 * n + 256)
        qkv_s[:, cols] = dot(tokw[...], wqkv[:, cols]).astype(BF16)
    for n in range(2):
        cols = slice(256 * n, 256 * n + 256)
        da_s[:, cols] = dot(cotw[...], wproj[cols], NT).astype(BF16)

    chan = lax.broadcasted_iota(jnp.int32, (PAD, 128), 1) // HD
    none = jnp.zeros((PAD, 128), BF16)

    def spread(v):
        return jnp.concatenate([jnp.where(chan == h, v, none) for h in range(4)], axis=0)

    def fold(full):
        total = full[0:PAD]
        for h in range(1, 4):
            total = jnp.where(chan == h, full[h * PAD : (h + 1) * PAD], total)
        return total.astype(BF16)

    def scores(rows, mask, g):
        cq = slice(g * 128, g * 128 + 128)
        k = qkv_s[rows, D + g * 128 : D + g * 128 + 128]
        v = qkv_s[rows, 2 * D + g * 128 : 2 * D + g * 128 + 128]
        qd = spread(qkv_s[rows, cq])
        dd = spread(da_s[rows, cq])
        return dict(rows=rows, mask=mask, g=g, k=k, v=v, qd=qd, dd=dd, s=dot(k, qd, NT), dp=dot(v, dd, NT))

    def softmax(it):
        g, mask = it["g"], it["mask"]
        bias = jnp.concatenate(
            [bias_s[2 * g * PAD : (2 * g + 1) * PAD] + mask, bias_s[(2 * g + 1) * PAD : (2 * g + 2) * PAD] + mask], axis=1
        )
        s = it["s"] * (scale * factor) + bias
        p = jnp.exp2(s - jnp.max(s, axis=0, keepdims=True))
        p = p * (1.0 / jnp.sum(p, axis=0, keepdims=True))
        dp = it["dp"].astype(BF16).astype(F32)
        ds = p * (dp - jnp.sum(dp * p, axis=0, keepdims=True))
        it["pb"] = p.astype(BF16)
        it["dsb"] = (ds * scale).astype(BF16)
        it["pt"] = jnp.transpose(it["pb"])
        it["dst"] = jnp.transpose(it["dsb"])
        return ds

    def results(it):
        rows, g = it["rows"], it["g"]
        cq = slice(g * 128, g * 128 + 128)
        dqkv_s[rows, 2 * D + g * 128 : 2 * D + g * 128 + 128] = dot(it["pb"], it["dd"]).astype(BF16)
        att_s[rows, cq] = fold(dot(it["pt"], it["v"]))
        dqkv_s[rows, D + g * 128 : D + g * 128 + 128] = dot(it["dsb"], it["qd"]).astype(BF16)
        dqkv_s[rows, cq] = fold(dot(it["dst"], it["k"]))

    def windows(step, carry):
        chains = []
        for g in range(4):
            for i in range(UNROLL):
                rows = pl.ds(pl.multiple_of((step * UNROLL + i) * PAD, PAD), PAD)
                chains.append((rows, i, g))
        masks = [mask_s[pl.ds(pl.multiple_of((step * UNROLL + i) * PAD, PAD), PAD), :] for i in range(UNROLL)]
        sums = [None] * 4
        items = []
        for c in range(len(chains) + 1 + AHEAD):
            if c < len(chains):
                rows, i, g = chains[c]
                items.append(scores(rows, masks[i], g))
            if 0 <= c - AHEAD < len(chains):
                it = items[c - AHEAD]
                ds = softmax(it)
                g = it["g"]
                sums[g] = ds if sums[g] is None else sums[g] + ds
                if c - AHEAD == UNROLL * g + UNROLL - 1:
                    acc_s[2 * g * PAD : (2 * g + 1) * PAD] += sums[g][:, 0:128]
                    acc_s[(2 * g + 1) * PAD : (2 * g + 2) * PAD] += sums[g][:, 128:256]
            if c - AHEAD - 1 >= 0:
                results(items[c - AHEAD - 1])
        return carry

    lax.fori_loop(0, WIN // UNROLL, windows, 0)

    ent = lax.broadcasted_iota(jnp.int32, (EPAD, 128), 0)
    sums = jnp.zeros((EPAD, 32), F32)
    left = lax.broadcasted_iota(jnp.int32, (8, 128), 1) < 64
    for j7 in range(7):
        hots, parts = [], []
        for j in range(7 * j7, 7 * j7 + 7):
            part = acc_s[pl.ds(j, 8, stride=PAD), :]
            top = part.astype(BF16).astype(F32)
            rest = part - top
            split = [jnp.where(left, top, 0.0), jnp.where(left, rest, 0.0), jnp.where(left, 0.0, top), jnp.where(left, 0.0, rest)]
            parts.append(jnp.concatenate(split, axis=0).astype(BF16))
            hots.append(jnp.where(ent == relt[j : j + 1], 1.0, 0.0).astype(BF16))
        sums = sums + dot(jnp.concatenate(hots, axis=1), jnp.concatenate(parts, axis=1), NT)
    sums = jnp.concatenate([sums, jnp.zeros((EPAD, 96), F32)], axis=1)
    sums = jnp.concatenate([sums, pltpu.roll(sums, 112, 1), jnp.zeros((384 - 2 * EPAD, 128), F32)], axis=0)
    flat = jnp.concatenate([jnp.transpose(sums[128 * k : 128 * k + 128])[0:16] for k in range(3)], axis=1)
    table = flat[0:8] + flat[8:16]
    for k in range(3):
        keep[4096 + 8 * k : 4104 + 8 * k] = table[:, 128 * k : 128 * k + 128]
        send[4096 + 8 * k : 4104 + 8 * k] = table[:, 128 * k : 128 * k + 128]

    core = lax.axis_index("gz") & 1

    def put(grad, block):
        for half in range(2):
            cols = slice(128 * half, 128 * half + 128)
            for k in range(16):
                at = 256 * k + 16 * (block + half)
                keep[at : at + 16] = grad[16 * k : 16 * k + 16, cols]
                send[at : at + 16] = grad[256 + 16 * k : 272 + 16 * k, cols]

    reorder(core, tokw, t_s)
    for n in range(6):
        put(dot(t_s[...], dqkv_s[:, 256 * n : 256 * n + 256]), 2 * n)
    reorder(core, att_s, t_s)
    for n in range(2):
        put(dot(t_s[...], cotw[:, 256 * n : 256 * n + 256]), 12 + 2 * n)


def place():
    gx, gz = lax.axis_index("gx"), lax.axis_index("gz")
    return gx & 3, ((gx >> 2) << 1) + (gz >> 1)


def block(index, size):
    return pl.ds(pl.multiple_of(index * size, size), size)


def by_offset(refs):
    return [[refs[2 * OFFSETS.index(k) + half] for k in range(4)] for half in range(2)]


def sum_core(keep, got, *outs):
    one, two = by_offset(outs)
    x, y = place()
    table = keep[4096:4120] + got[4096:4120]
    for k in range(4):
        for other in range(4):
            rows = slice(128 * other, 128 * other + 128)
            at = block(2 * (4 * other + ((x + k) & 3)), 128)
            one[k][rows] = keep[at] + got[at]
            at = block(2 * (4 * ((y + k) & 3) + other) + 1, 128)
            two[k][rows] = keep[at] + got[at]
        one[k][512:536] = table


def four(refs, rows):
    return (refs[0][rows] + refs[2][rows]) + (refs[1][rows] + refs[3][rows])


def sum_first(*refs):
    (a, b), (one, two) = by_offset(refs[0:8]), by_offset(refs[8:16])
    x, y = place()
    table = four(a, slice(512, 536))
    for k in range(4):
        one[k][0:128] = four(a, block((y + k) & 3, 128))
        one[k][128:152] = table
        two[k][...] = four(b, block((x + k) & 3, 128))


def sum_second(*refs):
    (a, b), out = by_offset(refs[0:8]), refs[8]
    for n in range(16):
        rows = slice(16 * (n % 8), 16 * (n % 8) + 16)
        part = four(a if n < 8 else b, rows)
        for z in range(8):
            out[z, 2 * n : 2 * n + 2] = part[2 * z : 2 * z + 2]
    table = four(a, slice(128, 152))
    for z in range(8):
        out[z, 32:56] = table


def finish(got, mq, mp, mt, oq, op, ot):
    total = got[0]
    for k in range(1, 8):
        total = total + got[k]
    total = total * (1.0 / 4096)
    for e in range(2):
        for c in range(12):
            row = 2 * c + e
            r = slice(12 * e + c, 12 * e + c + 1)
            oq[r] = 0.9 * mq[r] + total[row : row + 1]
        for c in range(4):
            row = 2 * (12 + c) + e
            r = slice(4 * e + c, 4 * e + c + 1)
            op[r] = 0.9 * mp[r] + total[row : row + 1]
    table = jnp.concatenate([total[32:40], total[40:48], total[48:56]], axis=1)
    for h in range(HEADS):
        at = (h % 2) * EPAD
        ot[h : h + 1] = 0.9 * mt[h : h + 1] + table[h // 2 : h // 2 + 1, at : at + ENT]


def shapes(*dims):
    return tuple(jax.ShapeDtypeStruct(d, F32) for d in dims)


def local_grads(tok, cot, regions, rel_index, w_qkv, w_proj, table, interpret=False):
    return pl.pallas_call(
        local_kernel,
        out_shape=shapes((4120, 128), (4120, 128)),
        in_specs=[pl.BlockSpec(memory_space=pltpu.HBM)] * 7,
        scratch_shapes=[
            pltpu.VMEM((ROWS, D), BF16),
            pltpu.VMEM((ROWS, D), BF16),
            pltpu.VMEM((WIN, TOK), jnp.int32),
            pltpu.VMEM((TOK, TOK), jnp.int32),
            pltpu.VMEM((D, 3 * D), BF16),
            pltpu.VMEM((D, D), BF16),
            pltpu.VMEM((HEADS, ENT), F32),
            pltpu.SemaphoreType.DMA((7,)),
            pltpu.VMEM((PROWS, D), BF16),
            pltpu.VMEM((PROWS, D), BF16),
            pltpu.VMEM((PROWS, 3 * D), BF16),
            pltpu.VMEM((PROWS, D), BF16),
            pltpu.VMEM((PROWS, D), BF16),
            pltpu.VMEM((PROWS, 3 * D), BF16),
            pltpu.VMEM((8 * PAD, 128), F32),
            pltpu.VMEM((WIN * PAD, 128), F32),
            pltpu.VMEM((8 * PAD, 128), F32),
            pltpu.VMEM((128, 128), F32),
            pltpu.VMEM((D, PROWS), BF16),
        ],
        name="local_grads",
        compiler_params=pltpu.CompilerParams(vmem_limit_bytes=40 << 20),
        interpret=interpret,
    )(*(pltpu.with_memory_space_constraint(v, pltpu.HBM) for v in (tok, cot, regions, rel_index, w_qkv, w_proj, table)))


def small(kernel, out_shape, *args):
    return pl.pallas_call(
        kernel, out_shape=out_shape, compiler_params=pltpu.CompilerParams(vmem_limit_bytes=3 << 20)
    )(*args)


def spread_out(m, one, two):
    out = list(m)
    for n in range(6):
        out[n] = shift(m[n], **{(one, two)[n % 2]: OFFSETS[n // 2]})
    return out


def body(
    tokens, cotangent, regions, rel_index, w_qkv, w_proj, bias_table, mom_qkv, mom_proj, mom_table
):
    tok = jnp.transpose(tokens, (1, 0, 2)).reshape(ROWS, D)
    cot = jnp.transpose(cotangent, (1, 0, 2)).reshape(ROWS, D)
    keep, send = local_grads(tok, cot, regions, rel_index, w_qkv, w_proj, bias_table.T)
    got = shift(send, dc=1)
    m = small(sum_core, shapes(*[(536, 128), (512, 128)] * 4), keep, got)
    m = spread_out(m, "dx", "dy")
    m = small(sum_first, shapes(*[(152, 128), (128, 128)] * 4), *m)
    m = spread_out(m, "dy", "dx")
    line = small(sum_second, jax.ShapeDtypeStruct((8, 56, 128), F32), *m)
    line = lax.all_to_all(line, "gy", 0, 0, tiled=True)
    new_q, new_p, new_t = small(
        finish,
        shapes((24, 128), (8, 128), (HEADS, ENT)),
        line,
        mom_qkv.reshape(24, 128),
        mom_proj.reshape(8, 128),
        mom_table.T,
    )
    return new_q.reshape(-1), new_p.reshape(-1), new_t.T


def solution(mesh):
    return jax.shard_map(
        body,
        mesh=mesh,
        in_specs=(
            P(AXES, None, None),
            P(AXES, None, None),
            P(AXES, None),
            P(),
            P(),
            P(),
            P(),
            P(AXES),
            P(AXES),
            P(),
        ),
        out_specs=(P(AXES), P(AXES), P()),
        check_vma=False,
    )
```

profile of v0, /device:TPU:6, one launch (start us, length us, event | category | flops | bytes accessed | tf_op | source)
XLA Modules:
  0.0 72.6 jit_solution(8344108625637905568)
XLA Ops:
  0.6 15.2 %local_grads.1 = (f32[4120,128]{1,0:T(8,128)S(1)}, f32[4120,128]{1,0:T(8,128)S(1)}) custom-call(bf16[784,512]{1,0:T(8,128)(2,1)} %bitcast.16, bf16[784,512]{1,0:T(8,128)(2,1)} %bitcast.17, s32[16,49]{1,0:T(8,128)} %reg_h.1, s32[49,49]{1,0:T(8,128)} %rel_h.1, bf16[512,1536]{1,0:T(8,128)(2,1)} %wqkv_h.1, bf16[512,512]{1,0:T(8,128)(2,1)} %wproj_h.1, ...), custom_call_target="tpu_custom_call" | custom-call | tf_op jit(solution)/shard_map/local_grads/pallas_call | solution.py:339
  15.8 0.1 collective-permute-start
  15.9 4.2 %collective-permute-done.got = f32[4120,128]{1,0:T(8,128)S(1)} collective-permute-done((f32[4120,128]{1,0:T(8,128)S(1)}, f32[4120,128]{1,0:T(8,128)S(1)}, u32[]{:S(2)}, u32[]{:S(2)}) %collective-permute-start) | collective-permute-done | bytes 2109472 | tf_op jit(solution)/shard_map/ppermute | solution.py:48
  20.1 0.2 shard_map.121
  20.3 0.0 copy-start
  20.3 0.0 copy-start.1
  20.3 0.0 copy-start.2
  20.3 3.3 %collective-permute-start.2 = (f32[512,128]{1,0:T(8,128)S(1)}, f32[512,128]{1,0:T(8,128)S(1)}, u32[]{:S(2)}, u32[]{:S(2)}) collective-permute-start(f32[512,128]{1,0:T(8,128)S(1)} %get-tuple-element.27), channel_id=1, source_target_pairs={{0,128},{1,129},{2,130},{3,131},{4,132},{5,133},{6,134},{7,135},{8... | collective-permute-start | bytes 786440 | tf_op jit(solution)/shard_map/ppermute | solution.py:48
  23.6 1.4 %collective-permute-start.1 = (f32[536,128]{1,0:T(8,128)S(1)}, f32[536,128]{1,0:T(8,128)S(1)}, u32[]{:S(2)}, u32[]{:S(2)}) collective-permute-start(f32[536,128]{1,0:T(8,128)S(1)} %get-tuple-element.26), channel_id=1, source_target_pairs={{0,64},{1,65},{2,66},{3,67},{4,68},{5,69},{6,70},{7,71},{8,72},{9,... | collective-permute-start | bytes 823304 | tf_op jit(solution)/shard_map/ppermute | solution.py:48
  25.0 2.1 %collective-permute-start.3 = (f32[536,128]{1,0:T(8,128)S(1)}, f32[536,128]{1,0:T(8,128)S(1)}, u32[]{:S(2)}, u32[]{:S(2)}) collective-permute-start(f32[536,128]{1,0:T(8,128)S(1)} %get-tuple-element.28), channel_id=1, source_target_pairs={{0,32},{1,33},{2,34},{3,35},{4,36},{5,37},{6,38},{7,39},{8,40},{9,... | collective-permute-start | bytes 823304 | tf_op jit(solution)/shard_map/ppermute | solution.py:48
  27.1 0.0 collective-permute-start.5
  27.1 0.7 collective-permute-start.4
  27.8 3.2 %collective-permute-done.2.refs_1_ = f32[512,128]{1,0:T(8,128)S(1)} collective-permute-done((f32[512,128]{1,0:T(8,128)S(1)}, f32[512,128]{1,0:T(8,128)S(1)}, u32[]{:S(2)}, u32[]{:S(2)}) %collective-permute-start.2) | collective-permute-done | bytes 262176 | tf_op jit(solution)/shard_map/ppermute | solution.py:48
  31.0 2.3 %collective-permute-start.6 = (f32[512,128]{1,0:T(8,128)S(1)}, f32[512,128]{1,0:T(8,128)S(1)}, u32[]{:S(2)}, u32[]{:S(2)}) collective-permute-start(f32[512,128]{1,0:T(8,128)S(1)} %get-tuple-element.31), channel_id=1, source_target_pairs={{0,130},{1,131},{2,0},{3,1},{4,134},{5,135},{6,4},{7,5},{8,138},{9... | collective-permute-start | bytes 786440 | tf_op jit(solution)/shard_map/ppermute | solution.py:48
  33.3 3.0 %collective-permute-done.4.refs_3_ = f32[512,128]{1,0:T(8,128)S(1)} collective-permute-done((f32[512,128]{1,0:T(8,128)S(1)}, f32[512,128]{1,0:T(8,128)S(1)}, u32[]{:S(2)}, u32[]{:S(2)}) %collective-permute-start.4) | collective-permute-done | bytes 262176 | tf_op jit(solution)/shard_map/ppermute | solution.py:48
  36.2 2.1 %collective-permute-done.6.refs_5_ = f32[512,128]{1,0:T(8,128)S(1)} collective-permute-done((f32[512,128]{1,0:T(8,128)S(1)}, f32[512,128]{1,0:T(8,128)S(1)}, u32[]{:S(2)}, u32[]{:S(2)}) %collective-permute-start.6) | collective-permute-done | bytes 262176 | tf_op jit(solution)/shard_map/ppermute | solution.py:48
  38.3 0.0 collective-permute-done.1.refs_0_
  38.3 0.0 collective-permute-done.3.refs_2_
  38.3 1.0 %collective-permute-done.5.refs_4_ = f32[536,128]{1,0:T(8,128)S(1)} collective-permute-done((f32[536,128]{1,0:T(8,128)S(1)}, f32[536,128]{1,0:T(8,128)S(1)}, u32[]{:S(2)}, u32[]{:S(2)}) %collective-permute-start.5) | collective-permute-done | bytes 274464 | tf_op jit(solution)/shard_map/ppermute | solution.py:48
  39.3 0.1 shard_map.122
  39.5 1.6 %collective-permute-start.8 = (f32[128,128]{1,0:T(8,128)S(1)}, f32[128,128]{1,0:T(8,128)S(1)}, u32[]{:S(2)}, u32[]{:S(2)}) collective-permute-start(f32[128,128]{1,0:T(8,128)S(1)} %get-tuple-element.35), channel_id=1, source_target_pairs={{0,64},{1,65},{2,66},{3,67},{4,68},{5,69},{6,70},{7,71},{8,72},{9,... | collective-permute-start | bytes 196616 | tf_op jit(solution)/shard_map/ppermute | solution.py:48
  41.0 1.6 %collective-permute-start.7 = (f32[152,128]{1,0:T(8,128)S(1)}, f32[152,128]{1,0:T(8,128)S(1)}, u32[]{:S(2)}, u32[]{:S(2)}) collective-permute-start(f32[152,128]{1,0:T(8,128)S(1)} %get-tuple-element.34), channel_id=1, source_target_pairs={{0,128},{1,129},{2,130},{3,131},{4,132},{5,133},{6,134},{7,135},{8... | collective-permute-start | bytes 233480 | tf_op jit(solution)/shard_map/ppermute | solution.py:48
  42.6 1.8 %collective-permute-start.9 = (f32[152,128]{1,0:T(8,128)S(1)}, f32[152,128]{1,0:T(8,128)S(1)}, u32[]{:S(2)}, u32[]{:S(2)}) collective-permute-start(f32[152,128]{1,0:T(8,128)S(1)} %get-tuple-element.36), channel_id=1, source_target_pairs={{0,2},{1,3},{2,128},{3,129},{4,6},{5,7},{6,132},{7,133},{8,10},{9,... | collective-permute-start | bytes 233480 | tf_op jit(solution)/shard_map/ppermute | solution.py:48
  44.5 1.4 %collective-permute-start.11 = (f32[152,128]{1,0:T(8,128)S(1)}, f32[152,128]{1,0:T(8,128)S(1)}, u32[]{:S(2)}, u32[]{:S(2)}) collective-permute-start(f32[152,128]{1,0:T(8,128)S(1)} %get-tuple-element.38), channel_id=1, source_target_pairs={{0,130},{1,131},{2,0},{3,1},{4,134},{5,135},{6,4},{7,5},{8,138},{9... | collective-permute-start | bytes 233480 | tf_op jit(solution)/shard_map/ppermute | solution.py:48
  45.9 2.1 %collective-permute-start.10 = (f32[128,128]{1,0:T(8,128)S(1)}, f32[128,128]{1,0:T(8,128)S(1)}, u32[]{:S(2)}, u32[]{:S(2)}) collective-permute-start(f32[128,128]{1,0:T(8,128)S(1)} %get-tuple-element.37), channel_id=1, source_target_pairs={{0,32},{1,33},{2,34},{3,35},{4,36},{5,37},{6,38},{7,39},{8,40},{9,... | collective-permute-start | bytes 196616 | tf_op jit(solution)/shard_map/ppermute | solution.py:48
  48.0 0.0 collective-permute-done.8.refs_1_
  48.0 0.0 collective-permute-start.12
  48.0 2.2 %collective-permute-done.10.refs_3_ = f32[128,128]{1,0:T(8,128)S(1)} collective-permute-done((f32[128,128]{1,0:T(8,128)S(1)}, f32[128,128]{1,0:T(8,128)S(1)}, u32[]{:S(2)}, u32[]{:S(2)}) %collective-permute-start.10) | collective-permute-done | bytes 65568 | tf_op jit(solution)/shard_map/ppermute | solution.py:48
  50.1 3.3 %collective-permute-done.12.refs_5_ = f32[128,128]{1,0:T(8,128)S(1)} collective-permute-done((f32[128,128]{1,0:T(8,128)S(1)}, f32[128,128]{1,0:T(8,128)S(1)}, u32[]{:S(2)}, u32[]{:S(2)}) %collective-permute-start.12) | collective-permute-done | bytes 65568 | tf_op jit(solution)/shard_map/ppermute | solution.py:48
  53.5 0.0 collective-permute-done.7.refs_0_
  53.5 0.0 collective-permute-done.9.refs_2_
  53.5 0.0 collective-permute-done.11.refs_4_
  53.5 0.1 shard_map.123
  53.5 18.4 %all_to_all.5.got = f32[8,56,128]{2,1,0:T(8,128)S(1)} all-to-all(f32[8,56,128]{2,1,0:T(8,128)S(1)} %shard_map.123), channel_id=1, replica_groups=mesh['gx'=8,'gy'=8,'gz'=4] {'gy'}, dimensions={0} | all-to-all | bytes 458752 | tf_op jit(solution)/shard_map/all_to_all | solution.py:395
  71.9 0.0 copy-done
  71.9 0.0 copy-done.1
  71.9 0.0 copy-done.2
  71.9 0.7 shard_map.124
Async XLA Ops:
  15.8 4.3 %collective-permute-start = (f32[4120,128]{1,0:T(8,128)S(1)}, f32[4120,128]{1,0:T(8,128)S(1)}, u32[]{:S(2)}, u32[]{:S(2)}) collective-permute-start(f32[4120,128]{1,0:T(8,128)S(1)} %get-tuple-element.25), channel_id=1, source_target_pairs={{0,1},{1,0},{2,3},{3,2},{4,5},{5,4},{6,7},{7,6},{8,9},{9,8},{10,11... | collective-permute-start | bytes 6328328 | tf_op jit(solution)/shard_map/ppermute | solution.py:48
  20.3 51.6 %copy-start = (f32[169,16]{0,1:T(8,128)S(1)}, f32[169,16]{0,1:T(8,128)}, u32[]{:S(2)}) copy-start(f32[169,16]{0,1:T(8,128)} %param.19) | copy-start | bytes 32452
  20.3 51.6 %copy-start.1 = (f32[3072]{0:T(1024)S(1)}, f32[3072]{0:T(1024)}, u32[]{:S(2)}) copy-start(f32[3072]{0:T(1024)} %param.17) | copy-start | bytes 36868
  20.3 51.6 %copy-start.2 = (f32[1024]{0:T(1024)S(1)}, f32[1024]{0:T(1024)}, u32[]{:S(2)}) copy-start(f32[1024]{0:T(1024)} %param.18) | copy-start | bytes 12292
  20.3 10.7 %collective-permute-start.2 = (f32[512,128]{1,0:T(8,128)S(1)}, f32[512,128]{1,0:T(8,128)S(1)}, u32[]{:S(2)}, u32[]{:S(2)}) collective-permute-start(f32[512,128]{1,0:T(8,128)S(1)} %get-tuple-element.27), channel_id=1, source_target_pairs={{0,128},{1,129},{2,130},{3,131},{4,132},{5,133},{6,134},{7,135},{8... | collective-permute-start | bytes 786440 | tf_op jit(solution)/shard_map/ppermute | solution.py:48
  23.6 14.7 %collective-permute-start.1 = (f32[536,128]{1,0:T(8,128)S(1)}, f32[536,128]{1,0:T(8,128)S(1)}, u32[]{:S(2)}, u32[]{:S(2)}) collective-permute-start(f32[536,128]{1,0:T(8,128)S(1)} %get-tuple-element.26), channel_id=1, source_target_pairs={{0,64},{1,65},{2,66},{3,67},{4,68},{5,69},{6,70},{7,71},{8,72},{9,... | collective-permute-start | bytes 823304 | tf_op jit(solution)/shard_map/ppermute | solution.py:48
  25.0 13.3 %collective-permute-start.3 = (f32[536,128]{1,0:T(8,128)S(1)}, f32[536,128]{1,0:T(8,128)S(1)}, u32[]{:S(2)}, u32[]{:S(2)}) collective-permute-start(f32[536,128]{1,0:T(8,128)S(1)} %get-tuple-element.28), channel_id=1, source_target_pairs={{0,32},{1,33},{2,34},{3,35},{4,36},{5,37},{6,38},{7,39},{8,40},{9,... | collective-permute-start | bytes 823304 | tf_op jit(solution)/shard_map/ppermute | solution.py:48
  27.1 12.2 %collective-permute-start.5 = (f32[536,128]{1,0:T(8,128)S(1)}, f32[536,128]{1,0:T(8,128)S(1)}, u32[]{:S(2)}, u32[]{:S(2)}) collective-permute-start(f32[536,128]{1,0:T(8,128)S(1)} %get-tuple-element.30), channel_id=1, source_target_pairs={{0,96},{1,97},{2,98},{3,99},{4,100},{5,101},{6,102},{7,103},{8,104... | collective-permute-start | bytes 823304 | tf_op jit(solution)/shard_map/ppermute | solution.py:48
  27.1 9.1 %collective-permute-start.4 = (f32[512,128]{1,0:T(8,128)S(1)}, f32[512,128]{1,0:T(8,128)S(1)}, u32[]{:S(2)}, u32[]{:S(2)}) collective-permute-start(f32[512,128]{1,0:T(8,128)S(1)} %get-tuple-element.29), channel_id=1, source_target_pairs={{0,2},{1,3},{2,128},{3,129},{4,6},{5,7},{6,132},{7,133},{8,10},{9,... | collective-permute-start | bytes 786440 | tf_op jit(solution)/shard_map/ppermute | solution.py:48
  31.0 7.3 %collective-permute-start.6 = (f32[512,128]{1,0:T(8,128)S(1)}, f32[512,128]{1,0:T(8,128)S(1)}, u32[]{:S(2)}, u32[]{:S(2)}) collective-permute-start(f32[512,128]{1,0:T(8,128)S(1)} %get-tuple-element.31), channel_id=1, source_target_pairs={{0,130},{1,131},{2,0},{3,1},{4,134},{5,135},{6,4},{7,5},{8,138},{9... | collective-permute-start | bytes 786440 | tf_op jit(solution)/shard_map/ppermute | solution.py:48
  39.5 8.5 %collective-permute-start.8 = (f32[128,128]{1,0:T(8,128)S(1)}, f32[128,128]{1,0:T(8,128)S(1)}, u32[]{:S(2)}, u32[]{:S(2)}) collective-permute-start(f32[128,128]{1,0:T(8,128)S(1)} %get-tuple-element.35), channel_id=1, source_target_pairs={{0,64},{1,65},{2,66},{3,67},{4,68},{5,69},{6,70},{7,71},{8,72},{9,... | collective-permute-start | bytes 196616 | tf_op jit(solution)/shard_map/ppermute | solution.py:48
  41.0 12.4 %collective-permute-start.7 = (f32[152,128]{1,0:T(8,128)S(1)}, f32[152,128]{1,0:T(8,128)S(1)}, u32[]{:S(2)}, u32[]{:S(2)}) collective-permute-start(f32[152,128]{1,0:T(8,128)S(1)} %get-tuple-element.34), channel_id=1, source_target_pairs={{0,128},{1,129},{2,130},{3,131},{4,132},{5,133},{6,134},{7,135},{8... | collective-permute-start | bytes 233480 | tf_op jit(solution)/shard_map/ppermute | solution.py:48
  42.6 10.8 %collective-permute-start.9 = (f32[152,128]{1,0:T(8,128)S(1)}, f32[152,128]{1,0:T(8,128)S(1)}, u32[]{:S(2)}, u32[]{:S(2)}) collective-permute-start(f32[152,128]{1,0:T(8,128)S(1)} %get-tuple-element.36), channel_id=1, source_target_pairs={{0,2},{1,3},{2,128},{3,129},{4,6},{5,7},{6,132},{7,133},{8,10},{9,... | collective-permute-start | bytes 233480 | tf_op jit(solution)/shard_map/ppermute | solution.py:48
  44.5 9.0 %collective-permute-start.11 = (f32[152,128]{1,0:T(8,128)S(1)}, f32[152,128]{1,0:T(8,128)S(1)}, u32[]{:S(2)}, u32[]{:S(2)}) collective-permute-start(f32[152,128]{1,0:T(8,128)S(1)} %get-tuple-element.38), channel_id=1, source_target_pairs={{0,130},{1,131},{2,0},{3,1},{4,134},{5,135},{6,4},{7,5},{8,138},{9... | collective-permute-start | bytes 233480 | tf_op jit(solution)/shard_map/ppermute | solution.py:48
  45.9 4.3 %collective-permute-start.10 = (f32[128,128]{1,0:T(8,128)S(1)}, f32[128,128]{1,0:T(8,128)S(1)}, u32[]{:S(2)}, u32[]{:S(2)}) collective-permute-start(f32[128,128]{1,0:T(8,128)S(1)} %get-tuple-element.37), channel_id=1, source_target_pairs={{0,32},{1,33},{2,34},{3,35},{4,36},{5,37},{6,38},{7,39},{8,40},{9,... | collective-permute-start | bytes 196616 | tf_op jit(solution)/shard_map/ppermute | solution.py:48
  48.0 5.5 %collective-permute-start.12 = (f32[128,128]{1,0:T(8,128)S(1)}, f32[128,128]{1,0:T(8,128)S(1)}, u32[]{:S(2)}, u32[]{:S(2)}) collective-permute-start(f32[128,128]{1,0:T(8,128)S(1)} %get-tuple-element.39), channel_id=1, source_target_pairs={{0,96},{1,97},{2,98},{3,99},{4,100},{5,101},{6,102},{7,103},{8,104... | collective-permute-start | bytes 196616 | tf_op jit(solution)/shard_map/ppermute | solution.py:48
where the time goes:
time: 72.8 us; the launch traced here: 72.6 us
  waiting for transfers between devices  18.9 us (26%)
  blocking collectives  18.4 us (25%)
  starting transfers between devices  18.3 us (25%)
  Pallas kernels  16.3 us (22%)
    ppermute x13, waiting for transfers between devices, shift(): return lax.ppermute(value, AXES, pairs)  18.9 us
    all_to_all x1, blocking collectives, body(): line = lax.all_to_all(line, 'gy', 0, 0, tiled=True)  18.4 us
    ppermute x13, starting transfers between devices, shift(): return lax.ppermute(value, AXES, pairs)  18.3 us
    pallas_call x1, Pallas kernels, local_grads(): pl.pallas_call(local_kernel, out_shape=shapes((4120, 128), (4120, 128)),...  15.2 us
  transfers between devices with their start and end apart: 13, of which 7 were waited for; matrix products, arithmetic and copies ran while one was open for 0% of the time, Pallas kernels for 0%

commit v1 on v0

--- a/solution.py
+++ b/solution.py
@@ -65,13 +65,13 @@
 
 
 def local_kernel(
-    tok_h, cot_h, reg_h, rel_h, wqkv_h, wproj_h, tab_h, keep, send,
+    tok_h, cot_h, reg_h, rel_h, wqkv_h, wproj_h, tab_h, keep1, keep2, send1, send2,
     tok, cot, reg, rel, wqkv, wproj, tab, sems, tokw, cotw, qkv_s, da_s, att_s, dqkv_s, bias_s, mask_s, acc_s, sq_s, t_s,
 ):
     moves = [
         pltpu.make_async_copy(src, dst, sems.at[n])
         for n, (src, dst) in enumerate(
-            zip((tok_h, rel_h, reg_h, tab_h, wqkv_h, cot_h, wproj_h), (tok, rel, reg, tab, wqkv, cot, wproj))
+            zip((rel_h, reg_h, tab_h, tok_h, wqkv_h, cot_h, wproj_h), (rel, reg, tab, tok, wqkv, cot, wproj))
         )
     ]
     for move in moves:
@@ -94,9 +94,8 @@
             for w in range(WIN):
                 dst[w * PAD + 16 * b : w * PAD + 16 * b + 16] = moved[16 * w : 16 * w + 16]
 
-    for move in moves[0:4]:
+    for move in moves[0:3]:
         move.wait()
-    regroup(tok, tokw)
 
     sq_s[...] = jnp.zeros((128, 128), F32)
     sq_s[0:TOK, 0:TOK] = rel[...].astype(F32)
@@ -138,8 +137,9 @@
 
     acc_s[...] = jnp.zeros(acc_s.shape, F32)
 
-    for move in moves[4:7]:
+    for move in moves[3:7]:
         move.wait()
+    regroup(tok, tokw)
     regroup(cot, cotw)
     for n in range(6):
         cols = slice(256 * n, 256 * n + 256)
@@ -237,16 +237,17 @@
     flat = jnp.concatenate([jnp.transpose(sums[128 * k : 128 * k + 128])[0:16] for k in range(3)], axis=1)
     table = flat[0:8] + flat[8:16]
     for k in range(3):
-        keep[4096 + 8 * k : 4104 + 8 * k] = table[:, 128 * k : 128 * k + 128]
-        send[4096 + 8 * k : 4104 + 8 * k] = table[:, 128 * k : 128 * k + 128]
+        keep1[2048 + 8 * k : 2056 + 8 * k] = table[:, 128 * k : 128 * k + 128]
+        send1[2048 + 8 * k : 2056 + 8 * k] = table[:, 128 * k : 128 * k + 128]
 
     core = lax.axis_index("gz") & 1
 
     def put(grad, block):
+        keep, send = (keep1, send1) if block < 8 else (keep2, send2)
         for half in range(2):
             cols = slice(128 * half, 128 * half + 128)
             for k in range(16):
-                at = 256 * k + 16 * (block + half)
+                at = 128 * k + 16 * (block % 8 + half)
                 keep[at : at + 16] = grad[16 * k : 16 * k + 16, cols]
                 send[at : at + 16] = grad[256 + 16 * k : 272 + 16 * k, cols]
 
@@ -271,18 +272,21 @@
     return [[refs[2 * OFFSETS.index(k) + half] for k in range(4)] for half in range(2)]
 
 
-def sum_core(keep, got, *outs):
-    one, two = by_offset(outs)
-    x, y = place()
-    table = keep[4096:4120] + got[4096:4120]
-    for k in range(4):
+def sum_core_x(keep, got, *outs):
+    x, _ = place()
+    for out, k in zip(outs, OFFSETS):
         for other in range(4):
-            rows = slice(128 * other, 128 * other + 128)
-            at = block(2 * (4 * other + ((x + k) & 3)), 128)
-            one[k][rows] = keep[at] + got[at]
-            at = block(2 * (4 * ((y + k) & 3) + other) + 1, 128)
-            two[k][rows] = keep[at] + got[at]
-        one[k][512:536] = table
+            at = block(4 * other + ((x + k) & 3), 128)
+            out[128 * other : 128 * other + 128] = keep[at] + got[at]
+        out[512:536] = keep[2048:2072] + got[2048:2072]
+
+
+def sum_core_y(keep, got, *outs):
+    _, y = place()
+    for out, k in zip(outs, OFFSETS):
+        for other in range(4):
+            at = block(4 * ((y + k) & 3) + other, 128)
+            out[128 * other : 128 * other + 128] = keep[at] + got[at]
 
 
 def four(refs, rows):
@@ -338,7 +342,7 @@
 def local_grads(tok, cot, regions, rel_index, w_qkv, w_proj, table, interpret=False):
     return pl.pallas_call(
         local_kernel,
-        out_shape=shapes((4120, 128), (4120, 128)),
+        out_shape=shapes((2072, 128), (2048, 128), (2072, 128), (2048, 128)),
         in_specs=[pl.BlockSpec(memory_space=pltpu.HBM)] * 7,
         scratch_shapes=[
             pltpu.VMEM((ROWS, D), BF16),
@@ -385,9 +389,12 @@
 ):
     tok = jnp.transpose(tokens, (1, 0, 2)).reshape(ROWS, D)
     cot = jnp.transpose(cotangent, (1, 0, 2)).reshape(ROWS, D)
-    keep, send = local_grads(tok, cot, regions, rel_index, w_qkv, w_proj, bias_table.T)
-    got = shift(send, dc=1)
-    m = small(sum_core, shapes(*[(536, 128), (512, 128)] * 4), keep, got)
+    keep1, keep2, send1, send2 = local_grads(tok, cot, regions, rel_index, w_qkv, w_proj, bias_table.T)
+    got1 = shift(send1, dc=1)
+    got2 = shift(send2, dc=1)
+    xs = small(sum_core_x, shapes(*[(536, 128)] * 4), keep1, got1)
+    ys = small(sum_core_y, shapes(*[(512, 128)] * 4), keep2, got2)
+    m = [v for pair in zip(xs, ys) for v in pair]
     m = spread_out(m, "dx", "dy")
     m = small(sum_first, shapes(*[(152, 128), (128, 128)] * 4), *m)
     m = spread_out(m, "dy", "dx")

time: 72.8 us -> 71.3 us (0.979)
  waiting for transfers between devices: 18.9 us -> 16.3 us
  starting transfers between devices: 18.3 us -> 19.3 us
    ppermute x13 -> x14, waiting for transfers between devices: 18.9 us -> 16.3 us  [shift(): return lax.ppermute(value, AXES, pairs)]
    ppermute x13 -> x14, starting transfers between devices: 18.3 us -> 19.3 us  [shift(): return lax.ppermute(value, AXES, pairs)]
  transfers between devices with their start and end apart: 13 -> 14, of which waited for: 7 -> 7; matrix products, arithmetic and copies ran while one was open for 0% -> 0% of each run, Pallas kernels for 0% -> 0%
where the time goes in v1:
time: 71.3 us; the launch traced here: 71.2 us
  starting transfers between devices  19.3 us (27%)
  blocking collectives  18.4 us (26%)
  Pallas kernels  16.5 us (23%)
  waiting for transfers between devices  16.3 us (23%)
    ppermute x14, starting transfers between devices, shift(): return lax.ppermute(value, AXES, pairs)  19.3 us
    all_to_all x1, blocking collectives, body(): line = lax.all_to_all(line, 'gy', 0, 0, tiled=True)  18.4 us
    ppermute x14, waiting for transfers between devices, shift(): return lax.ppermute(value, AXES, pairs)  16.3 us
    pallas_call x1, Pallas kernels, local_grads(): pl.pallas_call(local_kernel, out_shape=shapes((2072, 128), (2048, 128), (...  15.3 us
  transfers between devices with their start and end apart: 14, of which 7 were waited for; matrix products, arithmetic and copies ran while one was open for 0% of the time, Pallas kernels for 0%

profile of v1, /device:TPU:6, one launch (start us, length us, event | category | flops | bytes accessed | tf_op | source)
XLA Modules:
  0.0 71.2 jit_solution(14758214807347402293)
XLA Ops:
  0.6 15.3 %local_grads.1 = (f32[2072,128]{1,0:T(8,128)S(1)}, f32[2048,128]{1,0:T(8,128)S(1)}, f32[2072,128]{1,0:T(8,128)S(1)}, f32[2048,128]{1,0:T(8,128)S(1)}) custom-call(bf16[784,512]{1,0:T(8,128)(2,1)} %bitcast.16, bf16[784,512]{1,0:T(8,128)(2,1)} %bitcast.17, s32[16,49]{1,0:T(8,128)} %reg_h.1, s32[49,49]{1,0:T(8,128)} %rel_h.1, bf16[512,1536]{1,0:T(8,128)(2,1)} %wqkv_h.1, ...), custom_call_target="tpu_custom_call" | custom-call | tf_op jit(solution)/shard_map/local_grads/pallas_call | solution.py:343
  16.0 0.1 collective-permute-start.2
  16.1 0.5 collective-permute-start
  16.6 2.1 %collective-permute-done.2.got = f32[2048,128]{1,0:T(8,128)S(1)} collective-permute-done((f32[2048,128]{1,0:T(8,128)S(1)}, f32[2048,128]{1,0:T(8,128)S(1)}, u32[]{:S(2)}, u32[]{:S(2)}) %collective-permute-start.2) | collective-permute-done | bytes 1048608 | tf_op jit(solution)/shard_map/ppermute | solution.py:48
  18.7 0.2 shard_map.122
  18.9 3.3 %collective-permute-start.3 = (f32[512,128]{1,0:T(8,128)S(1)}, f32[512,128]{1,0:T(8,128)S(1)}, u32[]{:S(2)}, u32[]{:S(2)}) collective-permute-start(f32[512,128]{1,0:T(8,128)S(1)} %get-tuple-element.31), channel_id=1, source_target_pairs={{0,128},{1,129},{2,130},{3,131},{4,132},{5,133},{6,134},{7,135},{8... | collective-permute-start | bytes 786440 | tf_op jit(solution)/shard_map/ppermute | solution.py:48
  22.2 0.0 collective-permute-done.got
  22.2 0.1 shard_map.121
  22.3 1.5 %collective-permute-start.1 = (f32[536,128]{1,0:T(8,128)S(1)}, f32[536,128]{1,0:T(8,128)S(1)}, u32[]{:S(2)}, u32[]{:S(2)}) collective-permute-start(f32[536,128]{1,0:T(8,128)S(1)} %get-tuple-element.28), channel_id=1, source_target_pairs={{0,64},{1,65},{2,66},{3,67},{4,68},{5,69},{6,70},{7,71},{8,72},{9,... | collective-permute-start | bytes 823304 | tf_op jit(solution)/shard_map/ppermute | solution.py:48
  23.8 2.1 %collective-permute-start.4 = (f32[536,128]{1,0:T(8,128)S(1)}, f32[536,128]{1,0:T(8,128)S(1)}, u32[]{:S(2)}, u32[]{:S(2)}) collective-permute-start(f32[536,128]{1,0:T(8,128)S(1)} %get-tuple-element.32), channel_id=1, source_target_pairs={{0,32},{1,33},{2,34},{3,35},{4,36},{5,37},{6,38},{7,39},{8,40},{9,... | collective-permute-start | bytes 823304 | tf_op jit(solution)/shard_map/ppermute | solution.py:48
  25.9 0.0 collective-permute-start.6
  25.9 0.7 collective-permute-start.5
  26.6 2.5 %collective-permute-done.3.refs_1_ = f32[512,128]{1,0:T(8,128)S(1)} collective-permute-done((f32[512,128]{1,0:T(8,128)S(1)}, f32[512,128]{1,0:T(8,128)S(1)}, u32[]{:S(2)}, u32[]{:S(2)}) %collective-permute-start.3) | collective-permute-done | bytes 262176 | tf_op jit(solution)/shard_map/ppermute | solution.py:48
  29.0 2.8 %collective-permute-start.7 = (f32[512,128]{1,0:T(8,128)S(1)}, f32[512,128]{1,0:T(8,128)S(1)}, u32[]{:S(2)}, u32[]{:S(2)}) collective-permute-start(f32[512,128]{1,0:T(8,128)S(1)} %get-tuple-element.35), channel_id=1, source_target_pairs={{0,130},{1,131},{2,0},{3,1},{4,134},{5,135},{6,4},{7,5},{8,138},{9... | collective-permute-start | bytes 786440 | tf_op jit(solution)/shard_map/ppermute | solution.py:48
  31.8 2.8 %collective-permute-done.5.refs_3_ = f32[512,128]{1,0:T(8,128)S(1)} collective-permute-done((f32[512,128]{1,0:T(8,128)S(1)}, f32[512,128]{1,0:T(8,128)S(1)}, u32[]{:S(2)}, u32[]{:S(2)}) %collective-permute-start.5) | collective-permute-done | bytes 262176 | tf_op jit(solution)/shard_map/ppermute | solution.py:48
  34.6 2.2 %collective-permute-done.7.refs_5_ = f32[512,128]{1,0:T(8,128)S(1)} collective-permute-done((f32[512,128]{1,0:T(8,128)S(1)}, f32[512,128]{1,0:T(8,128)S(1)}, u32[]{:S(2)}, u32[]{:S(2)}) %collective-permute-start.7) | collective-permute-done | bytes 262176 | tf_op jit(solution)/shard_map/ppermute | solution.py:48
  36.8 0.0 collective-permute-done.1.refs_0_
  36.8 0.0 collective-permute-done.4.refs_2_
  36.8 1.3 %collective-permute-done.6.refs_4_ = f32[536,128]{1,0:T(8,128)S(1)} collective-permute-done((f32[536,128]{1,0:T(8,128)S(1)}, f32[536,128]{1,0:T(8,128)S(1)}, u32[]{:S(2)}, u32[]{:S(2)}) %collective-permute-start.6) | collective-permute-done | bytes 274464 | tf_op jit(solution)/shard_map/ppermute | solution.py:48
  38.1 0.1 shard_map.123
  38.2 0.0 copy-start
  38.2 0.0 copy-start.1
  38.3 0.0 copy-start.2
  38.3 1.6 %collective-permute-start.9 = (f32[128,128]{1,0:T(8,128)S(1)}, f32[128,128]{1,0:T(8,128)S(1)}, u32[]{:S(2)}, u32[]{:S(2)}) collective-permute-start(f32[128,128]{1,0:T(8,128)S(1)} %get-tuple-element.39), channel_id=1, source_target_pairs={{0,64},{1,65},{2,66},{3,67},{4,68},{5,69},{6,70},{7,71},{8,72},{9,... | collective-permute-start | bytes 196616 | tf_op jit(solution)/shard_map/ppermute | solution.py:48
  39.8 1.6 %collective-permute-start.8 = (f32[152,128]{1,0:T(8,128)S(1)}, f32[152,128]{1,0:T(8,128)S(1)}, u32[]{:S(2)}, u32[]{:S(2)}) collective-permute-start(f32[152,128]{1,0:T(8,128)S(1)} %get-tuple-element.38), channel_id=1, source_target_pairs={{0,128},{1,129},{2,130},{3,131},{4,132},{5,133},{6,134},{7,135},{8... | collective-permute-start | bytes 233480 | tf_op jit(solution)/shard_map/ppermute | solution.py:48
  41.4 1.7 %collective-permute-start.10 = (f32[152,128]{1,0:T(8,128)S(1)}, f32[152,128]{1,0:T(8,128)S(1)}, u32[]{:S(2)}, u32[]{:S(2)}) collective-permute-start(f32[152,128]{1,0:T(8,128)S(1)} %get-tuple-element.40), channel_id=1, source_target_pairs={{0,2},{1,3},{2,128},{3,129},{4,6},{5,7},{6,132},{7,133},{8,10},{9,... | collective-permute-start | bytes 233480 | tf_op jit(solution)/shard_map/ppermute | solution.py:48
  43.1 1.6 %collective-permute-start.12 = (f32[152,128]{1,0:T(8,128)S(1)}, f32[152,128]{1,0:T(8,128)S(1)}, u32[]{:S(2)}, u32[]{:S(2)}) collective-permute-start(f32[152,128]{1,0:T(8,128)S(1)} %get-tuple-element.42), channel_id=1, source_target_pairs={{0,130},{1,131},{2,0},{3,1},{4,134},{5,135},{6,4},{7,5},{8,138},{9... | collective-permute-start | bytes 233480 | tf_op jit(solution)/shard_map/ppermute | solution.py:48
  44.6 1.9 %collective-permute-start.11 = (f32[128,128]{1,0:T(8,128)S(1)}, f32[128,128]{1,0:T(8,128)S(1)}, u32[]{:S(2)}, u32[]{:S(2)}) collective-permute-start(f32[128,128]{1,0:T(8,128)S(1)} %get-tuple-element.41), channel_id=1, source_target_pairs={{0,32},{1,33},{2,34},{3,35},{4,36},{5,37},{6,38},{7,39},{8,40},{9,... | collective-permute-start | bytes 196616 | tf_op jit(solution)/shard_map/ppermute | solution.py:48
  46.6 0.0 collective-permute-done.9.refs_1_
  46.6 0.1 collective-permute-start.13
  46.7 2.2 %collective-permute-done.11.refs_3_ = f32[128,128]{1,0:T(8,128)S(1)} collective-permute-done((f32[128,128]{1,0:T(8,128)S(1)}, f32[128,128]{1,0:T(8,128)S(1)}, u32[]{:S(2)}, u32[]{:S(2)}) %collective-permute-start.11) | collective-permute-done | bytes 65568 | tf_op jit(solution)/shard_map/ppermute | solution.py:48
  48.9 3.1 %collective-permute-done.13.refs_5_ = f32[128,128]{1,0:T(8,128)S(1)} collective-permute-done((f32[128,128]{1,0:T(8,128)S(1)}, f32[128,128]{1,0:T(8,128)S(1)}, u32[]{:S(2)}, u32[]{:S(2)}) %collective-permute-start.13) | collective-permute-done | bytes 65568 | tf_op jit(solution)/shard_map/ppermute | solution.py:48
  52.0 0.0 collective-permute-done.8.refs_0_
  52.0 0.0 collective-permute-done.10.refs_2_
  52.0 0.0 collective-permute-done.12.refs_4_
  52.0 0.1 shard_map.124
  52.1 18.4 %all_to_all.5.got = f32[8,56,128]{2,1,0:T(8,128)S(1)} all-to-all(f32[8,56,128]{2,1,0:T(8,128)S(1)} %shard_map.124), channel_id=1, replica_groups=mesh['gx'=8,'gy'=8,'gz'=4] {'gy'}, dimensions={0} | all-to-all | bytes 458752 | tf_op jit(solution)/shard_map/all_to_all | solution.py:402
  70.5 0.0 copy-done
  70.5 0.0 copy-done.1
  70.5 0.0 copy-done.2
  70.5 0.7 shard_map.125
Async XLA Ops:
  16.0 2.7 %collective-permute-start.2 = (f32[2048,128]{1,0:T(8,128)S(1)}, f32[2048,128]{1,0:T(8,128)S(1)}, u32[]{:S(2)}, u32[]{:S(2)}) collective-permute-start(f32[2048,128]{1,0:T(8,128)S(1)} %get-tuple-element.30), channel_id=1, source_target_pairs={{0,1},{1,0},{2,3},{3,2},{4,5},{5,4},{6,7},{7,6},{8,9},{9,8},{10,11... | collective-permute-start | bytes 3145736 | tf_op jit(solution)/shard_map/ppermute | solution.py:48
  16.1 6.1 %collective-permute-start = (f32[2072,128]{1,0:T(8,128)S(1)}, f32[2072,128]{1,0:T(8,128)S(1)}, u32[]{:S(2)}, u32[]{:S(2)}) collective-permute-start(f32[2072,128]{1,0:T(8,128)S(1)} %get-tuple-element.27), channel_id=1, source_target_pairs={{0,1},{1,0},{2,3},{3,2},{4,5},{5,4},{6,7},{7,6},{8,9},{9,8},{10,11... | collective-permute-start | bytes 3182600 | tf_op jit(solution)/shard_map/ppermute | solution.py:48
  18.9 10.2 %collective-permute-start.3 = (f32[512,128]{1,0:T(8,128)S(1)}, f32[512,128]{1,0:T(8,128)S(1)}, u32[]{:S(2)}, u32[]{:S(2)}) collective-permute-start(f32[512,128]{1,0:T(8,128)S(1)} %get-tuple-element.31), channel_id=1, source_target_pairs={{0,128},{1,129},{2,130},{3,131},{4,132},{5,133},{6,134},{7,135},{8... | collective-permute-start | bytes 786440 | tf_op jit(solution)/shard_map/ppermute | solution.py:48
  22.3 14.5 %collective-permute-start.1 = (f32[536,128]{1,0:T(8,128)S(1)}, f32[536,128]{1,0:T(8,128)S(1)}, u32[]{:S(2)}, u32[]{:S(2)}) collective-permute-start(f32[536,128]{1,0:T(8,128)S(1)} %get-tuple-element.28), channel_id=1, source_target_pairs={{0,64},{1,65},{2,66},{3,67},{4,68},{5,69},{6,70},{7,71},{8,72},{9,... | collective-permute-start | bytes 823304 | tf_op jit(solution)/shard_map/ppermute | solution.py:48
  23.8 13.1 %collective-permute-start.4 = (f32[536,128]{1,0:T(8,128)S(1)}, f32[536,128]{1,0:T(8,128)S(1)}, u32[]{:S(2)}, u32[]{:S(2)}) collective-permute-start(f32[536,128]{1,0:T(8,128)S(1)} %get-tuple-element.32), channel_id=1, source_target_pairs={{0,32},{1,33},{2,34},{3,35},{4,36},{5,37},{6,38},{7,39},{8,40},{9,... | collective-permute-start | bytes 823304 | tf_op jit(solution)/shard_map/ppermute | solution.py:48
  25.9 12.2 %collective-permute-start.6 = (f32[536,128]{1,0:T(8,128)S(1)}, f32[536,128]{1,0:T(8,128)S(1)}, u32[]{:S(2)}, u32[]{:S(2)}) collective-permute-start(f32[536,128]{1,0:T(8,128)S(1)} %get-tuple-element.34), channel_id=1, source_target_pairs={{0,96},{1,97},{2,98},{3,99},{4,100},{5,101},{6,102},{7,103},{8,104... | collective-permute-start | bytes 823304 | tf_op jit(solution)/shard_map/ppermute | solution.py:48
  25.9 8.7 %collective-permute-start.5 = (f32[512,128]{1,0:T(8,128)S(1)}, f32[512,128]{1,0:T(8,128)S(1)}, u32[]{:S(2)}, u32[]{:S(2)}) collective-permute-start(f32[512,128]{1,0:T(8,128)S(1)} %get-tuple-element.33), channel_id=1, source_target_pairs={{0,2},{1,3},{2,128},{3,129},{4,6},{5,7},{6,132},{7,133},{8,10},{9,... | collective-permute-start | bytes 786440 | tf_op jit(solution)/shard_map/ppermute | solution.py:48
  29.0 7.8 %collective-permute-start.7 = (f32[512,128]{1,0:T(8,128)S(1)}, f32[512,128]{1,0:T(8,128)S(1)}, u32[]{:S(2)}, u32[]{:S(2)}) collective-permute-start(f32[512,128]{1,0:T(8,128)S(1)} %get-tuple-element.35), channel_id=1, source_target_pairs={{0,130},{1,131},{2,0},{3,1},{4,134},{5,135},{6,4},{7,5},{8,138},{9... | collective-permute-start | bytes 786440 | tf_op jit(solution)/shard_map/ppermute | solution.py:48
  38.2 32.3 %copy-start = (f32[169,16]{0,1:T(8,128)S(1)}, f32[169,16]{0,1:T(8,128)}, u32[]{:S(2)}) copy-start(f32[169,16]{0,1:T(8,128)} %param.19) | copy-start | bytes 32452
  38.2 32.3 %copy-start.1 = (f32[3072]{0:T(1024)S(1)}, f32[3072]{0:T(1024)}, u32[]{:S(2)}) copy-start(f32[3072]{0:T(1024)} %param.17) | copy-start | bytes 36868
  38.3 32.2 %copy-start.2 = (f32[1024]{0:T(1024)S(1)}, f32[1024]{0:T(1024)}, u32[]{:S(2)}) copy-start(f32[1024]{0:T(1024)} %param.18) | copy-start | bytes 12292
  38.3 8.3 %collective-permute-start.9 = (f32[128,128]{1,0:T(8,128)S(1)}, f32[128,128]{1,0:T(8,128)S(1)}, u32[]{:S(2)}, u32[]{:S(2)}) collective-permute-start(f32[128,128]{1,0:T(8,128)S(1)} %get-tuple-element.39), channel_id=1, source_target_pairs={{0,64},{1,65},{2,66},{3,67},{4,68},{5,69},{6,70},{7,71},{8,72},{9,... | collective-permute-start | bytes 196616 | tf_op jit(solution)/shard_map/ppermute | solution.py:48
  39.8 12.2 %collective-permute-start.8 = (f32[152,128]{1,0:T(8,128)S(1)}, f32[152,128]{1,0:T(8,128)S(1)}, u32[]{:S(2)}, u32[]{:S(2)}) collective-permute-start(f32[152,128]{1,0:T(8,128)S(1)} %get-tuple-element.38), channel_id=1, source_target_pairs={{0,128},{1,129},{2,130},{3,131},{4,132},{5,133},{6,134},{7,135},{8... | collective-permute-start | bytes 233480 | tf_op jit(solution)/shard_map/ppermute | solution.py:48
  41.4 10.6 %collective-permute-start.10 = (f32[152,128]{1,0:T(8,128)S(1)}, f32[152,128]{1,0:T(8,128)S(1)}, u32[]{:S(2)}, u32[]{:S(2)}) collective-permute-start(f32[152,128]{1,0:T(8,128)S(1)} %get-tuple-element.40), channel_id=1, source_target_pairs={{0,2},{1,3},{2,128},{3,129},{4,6},{5,7},{6,132},{7,133},{8,10},{9,... | collective-permute-start | bytes 233480 | tf_op jit(solution)/shard_map/ppermute | solution.py:48
  43.1 9.0 %collective-permute-start.12 = (f32[152,128]{1,0:T(8,128)S(1)}, f32[152,128]{1,0:T(8,128)S(1)}, u32[]{:S(2)}, u32[]{:S(2)}) collective-permute-start(f32[152,128]{1,0:T(8,128)S(1)} %get-tuple-element.42), channel_id=1, source_target_pairs={{0,130},{1,131},{2,0},{3,1},{4,134},{5,135},{6,4},{7,5},{8,138},{9... | collective-permute-start | bytes 233480 | tf_op jit(solution)/shard_map/ppermute | solution.py:48
  44.6 4.3 %collective-permute-start.11 = (f32[128,128]{1,0:T(8,128)S(1)}, f32[128,128]{1,0:T(8,128)S(1)}, u32[]{:S(2)}, u32[]{:S(2)}) collective-permute-start(f32[128,128]{1,0:T(8,128)S(1)} %get-tuple-element.41), channel_id=1, source_target_pairs={{0,32},{1,33},{2,34},{3,35},{4,36},{5,37},{6,38},{7,39},{8,40},{9,... | collective-permute-start | bytes 196616 | tf_op jit(solution)/shard_map/ppermute | solution.py:48
  46.6 5.5 %collective-permute-start.13 = (f32[128,128]{1,0:T(8,128)S(1)}, f32[128,128]{1,0:T(8,128)S(1)}, u32[]{:S(2)}, u32[]{:S(2)}) collective-permute-start(f32[128,128]{1,0:T(8,128)S(1)} %get-tuple-element.43), channel_id=1, source_target_pairs={{0,96},{1,97},{2,98},{3,99},{4,100},{5,101},{6,102},{7,103},{8,104... | collective-permute-start | bytes 196616 | tf_op jit(solution)/shard_map/ppermute | solution.py:48

commit v2 on v1

--- a/solution.py
+++ b/solution.py
@@ -66,7 +66,7 @@
 
 def local_kernel(
     tok_h, cot_h, reg_h, rel_h, wqkv_h, wproj_h, tab_h, keep1, keep2, send1, send2,
-    tok, cot, reg, rel, wqkv, wproj, tab, sems, tokw, cotw, qkv_s, da_s, att_s, dqkv_s, bias_s, mask_s, acc_s, sq_s, t_s,
+    tok, cot, reg, rel, wqkv, wproj, tab, sems, tokw, cotw, qkv_s, da_s, att_s, dqkv_s, bias_s, mask_s, acc_s, sq_s, t_s, u_s,
 ):
     moves = [
         pltpu.make_async_copy(src, dst, sems.at[n])
@@ -94,8 +94,11 @@
             for w in range(WIN):
                 dst[w * PAD + 16 * b : w * PAD + 16 * b + 16] = moved[16 * w : 16 * w + 16]
 
-    for move in moves[0:3]:
+    for move in moves[0:4]:
         move.wait()
+    core = lax.axis_index("gz") & 1
+    regroup(tok, tokw)
+    reorder(core, tokw, t_s)
 
     sq_s[...] = jnp.zeros((128, 128), F32)
     sq_s[0:TOK, 0:TOK] = rel[...].astype(F32)
@@ -137,13 +140,13 @@
 
     acc_s[...] = jnp.zeros(acc_s.shape, F32)
 
-    for move in moves[3:7]:
-        move.wait()
-    regroup(tok, tokw)
-    regroup(cot, cotw)
+    moves[4].wait()
     for n in range(6):
         cols = slice(256 * n, 256 * n + 256)
         qkv_s[:, cols] = dot(tokw[...], wqkv[:, cols]).astype(BF16)
+    for move in moves[5:7]:
+        move.wait()
+    regroup(cot, cotw)
     for n in range(2):
         cols = slice(256 * n, 256 * n + 256)
         da_s[:, cols] = dot(cotw[...], wproj[cols], NT).astype(BF16)
@@ -240,7 +243,6 @@
         keep1[2048 + 8 * k : 2056 + 8 * k] = table[:, 128 * k : 128 * k + 128]
         send1[2048 + 8 * k : 2056 + 8 * k] = table[:, 128 * k : 128 * k + 128]
 
-    core = lax.axis_index("gz") & 1
 
     def put(grad, block):
         keep, send = (keep1, send1) if block < 8 else (keep2, send2)
@@ -251,12 +253,11 @@
                 keep[at : at + 16] = grad[16 * k : 16 * k + 16, cols]
                 send[at : at + 16] = grad[256 + 16 * k : 272 + 16 * k, cols]
 
-    reorder(core, tokw, t_s)
     for n in range(6):
         put(dot(t_s[...], dqkv_s[:, 256 * n : 256 * n + 256]), 2 * n)
-    reorder(core, att_s, t_s)
+    reorder(core, att_s, u_s)
     for n in range(2):
-        put(dot(t_s[...], cotw[:, 256 * n : 256 * n + 256]), 12 + 2 * n)
+        put(dot(u_s[...], cotw[:, 256 * n : 256 * n + 256]), 12 + 2 * n)
 
 
 def place():
@@ -364,6 +365,7 @@
             pltpu.VMEM((8 * PAD, 128), F32),
             pltpu.VMEM((128, 128), F32),
             pltpu.VMEM((D, PROWS), BF16),
+            pltpu.VMEM((D, PROWS), BF16),
         ],
         name="local_grads",
         compiler_params=pltpu.CompilerParams(vmem_limit_bytes=40 << 20),

time: 71.3 us -> 71.1 us (level)
  no operation moved by 1% of the time
where the time goes in v2:
time: 71.1 us; the launch traced here: 70.9 us
  starting transfers between devices  19.3 us (27%)
  blocking collectives  18.4 us (26%)
  waiting for transfers between devices  16.3 us (23%)
  Pallas kernels  16.2 us (23%)
    ppermute x14, starting transfers between devices, shift(): return lax.ppermute(value, AXES, pairs)  19.3 us
    all_to_all x1, blocking collectives, body(): line = lax.all_to_all(line, 'gy', 0, 0, tiled=True)  18.4 us
    ppermute x14, waiting for transfers between devices, shift(): return lax.ppermute(value, AXES, pairs)  16.3 us
    pallas_call x1, Pallas kernels, local_grads(): pl.pallas_call(local_kernel, out_shape=shapes((2072, 128), (2048, 128), (...  15.1 us
  transfers between devices with their start and end apart: 14, of which 7 were waited for; matrix products, arithmetic and copies ran while one was open for 0% of the time, Pallas kernels for 0%

profile of v2, /device:TPU:6, one launch (start us, length us, event | category | flops | bytes accessed | tf_op | source)
XLA Modules:
  0.0 70.9 jit_solution(4629735472481157325)
XLA Ops:
  0.6 15.1 %local_grads.1 = (f32[2072,128]{1,0:T(8,128)S(1)}, f32[2048,128]{1,0:T(8,128)S(1)}, f32[2072,128]{1,0:T(8,128)S(1)}, f32[2048,128]{1,0:T(8,128)S(1)}) custom-call(bf16[784,512]{1,0:T(8,128)(2,1)} %bitcast.16, bf16[784,512]{1,0:T(8,128)(2,1)} %bitcast.17, s32[16,49]{1,0:T(8,128)} %reg_h.1, s32[49,49]{1,0:T(8,128)} %rel_h.1, bf16[512,1536]{1,0:T(8,128)(2,1)} %wqkv_h.1, ...), custom_call_target="tpu_custom_call" | custom-call | tf_op jit(solution)/shard_map/local_grads/pallas_call | solution.py:344
  15.7 0.1 collective-permute-start.2
  15.8 0.5 collective-permute-start
  16.3 2.1 %collective-permute-done.2.got = f32[2048,128]{1,0:T(8,128)S(1)} collective-permute-done((f32[2048,128]{1,0:T(8,128)S(1)}, f32[2048,128]{1,0:T(8,128)S(1)}, u32[]{:S(2)}, u32[]{:S(2)}) %collective-permute-start.2) | collective-permute-done | bytes 1048608 | tf_op jit(solution)/shard_map/ppermute | solution.py:48
  18.4 0.2 shard_map.122
  18.6 3.3 %collective-permute-start.3 = (f32[512,128]{1,0:T(8,128)S(1)}, f32[512,128]{1,0:T(8,128)S(1)}, u32[]{:S(2)}, u32[]{:S(2)}) collective-permute-start(f32[512,128]{1,0:T(8,128)S(1)} %get-tuple-element.31), channel_id=1, source_target_pairs={{0,128},{1,129},{2,130},{3,131},{4,132},{5,133},{6,134},{7,135},{8... | collective-permute-start | bytes 786440 | tf_op jit(solution)/shard_map/ppermute | solution.py:48
  21.9 0.0 collective-permute-done.got
  21.9 0.1 shard_map.121
  22.0 1.5 %collective-permute-start.1 = (f32[536,128]{1,0:T(8,128)S(1)}, f32[536,128]{1,0:T(8,128)S(1)}, u32[]{:S(2)}, u32[]{:S(2)}) collective-permute-start(f32[536,128]{1,0:T(8,128)S(1)} %get-tuple-element.28), channel_id=1, source_target_pairs={{0,64},{1,65},{2,66},{3,67},{4,68},{5,69},{6,70},{7,71},{8,72},{9,... | collective-permute-start | bytes 823304 | tf_op jit(solution)/shard_map/ppermute | solution.py:48
  23.5 2.1 %collective-permute-start.4 = (f32[536,128]{1,0:T(8,128)S(1)}, f32[536,128]{1,0:T(8,128)S(1)}, u32[]{:S(2)}, u32[]{:S(2)}) collective-permute-start(f32[536,128]{1,0:T(8,128)S(1)} %get-tuple-element.32), channel_id=1, source_target_pairs={{0,32},{1,33},{2,34},{3,35},{4,36},{5,37},{6,38},{7,39},{8,40},{9,... | collective-permute-start | bytes 823304 | tf_op jit(solution)/shard_map/ppermute | solution.py:48
  25.6 0.0 collective-permute-start.6
  25.6 0.7 collective-permute-start.5
  26.3 2.5 %collective-permute-done.3.refs_1_ = f32[512,128]{1,0:T(8,128)S(1)} collective-permute-done((f32[512,128]{1,0:T(8,128)S(1)}, f32[512,128]{1,0:T(8,128)S(1)}, u32[]{:S(2)}, u32[]{:S(2)}) %collective-permute-start.3) | collective-permute-done | bytes 262176 | tf_op jit(solution)/shard_map/ppermute | solution.py:48
  28.8 2.8 %collective-permute-start.7 = (f32[512,128]{1,0:T(8,128)S(1)}, f32[512,128]{1,0:T(8,128)S(1)}, u32[]{:S(2)}, u32[]{:S(2)}) collective-permute-start(f32[512,128]{1,0:T(8,128)S(1)} %get-tuple-element.35), channel_id=1, source_target_pairs={{0,130},{1,131},{2,0},{3,1},{4,134},{5,135},{6,4},{7,5},{8,138},{9... | collective-permute-start | bytes 786440 | tf_op jit(solution)/shard_map/ppermute | solution.py:48
  31.5 2.8 %collective-permute-done.5.refs_3_ = f32[512,128]{1,0:T(8,128)S(1)} collective-permute-done((f32[512,128]{1,0:T(8,128)S(1)}, f32[512,128]{1,0:T(8,128)S(1)}, u32[]{:S(2)}, u32[]{:S(2)}) %collective-permute-start.5) | collective-permute-done | bytes 262176 | tf_op jit(solution)/shard_map/ppermute | solution.py:48
  34.4 2.2 %collective-permute-done.7.refs_5_ = f32[512,128]{1,0:T(8,128)S(1)} collective-permute-done((f32[512,128]{1,0:T(8,128)S(1)}, f32[512,128]{1,0:T(8,128)S(1)}, u32[]{:S(2)}, u32[]{:S(2)}) %collective-permute-start.7) | collective-permute-done | bytes 262176 | tf_op jit(solution)/shard_map/ppermute | solution.py:48
  36.6 0.0 collective-permute-done.1.refs_0_
  36.6 0.0 collective-permute-done.4.refs_2_
  36.6 1.3 %collective-permute-done.6.refs_4_ = f32[536,128]{1,0:T(8,128)S(1)} collective-permute-done((f32[536,128]{1,0:T(8,128)S(1)}, f32[536,128]{1,0:T(8,128)S(1)}, u32[]{:S(2)}, u32[]{:S(2)}) %collective-permute-start.6) | collective-permute-done | bytes 274464 | tf_op jit(solution)/shard_map/ppermute | solution.py:48
  37.8 0.1 shard_map.123
  38.0 0.0 copy-start
  38.0 0.0 copy-start.1
  38.0 0.0 copy-start.2
  38.0 1.6 %collective-permute-start.9 = (f32[128,128]{1,0:T(8,128)S(1)}, f32[128,128]{1,0:T(8,128)S(1)}, u32[]{:S(2)}, u32[]{:S(2)}) collective-permute-start(f32[128,128]{1,0:T(8,128)S(1)} %get-tuple-element.39), channel_id=1, source_target_pairs={{0,64},{1,65},{2,66},{3,67},{4,68},{5,69},{6,70},{7,71},{8,72},{9,... | collective-permute-start | bytes 196616 | tf_op jit(solution)/shard_map/ppermute | solution.py:48
  39.6 1.6 %collective-permute-start.8 = (f32[152,128]{1,0:T(8,128)S(1)}, f32[152,128]{1,0:T(8,128)S(1)}, u32[]{:S(2)}, u32[]{:S(2)}) collective-permute-start(f32[152,128]{1,0:T(8,128)S(1)} %get-tuple-element.38), channel_id=1, source_target_pairs={{0,128},{1,129},{2,130},{3,131},{4,132},{5,133},{6,134},{7,135},{8... | collective-permute-start | bytes 233480 | tf_op jit(solution)/shard_map/ppermute | solution.py:48
  41.1 1.7 %collective-permute-start.10 = (f32[152,128]{1,0:T(8,128)S(1)}, f32[152,128]{1,0:T(8,128)S(1)}, u32[]{:S(2)}, u32[]{:S(2)}) collective-permute-start(f32[152,128]{1,0:T(8,128)S(1)} %get-tuple-element.40), channel_id=1, source_target_pairs={{0,2},{1,3},{2,128},{3,129},{4,6},{5,7},{6,132},{7,133},{8,10},{9,... | collective-permute-start | bytes 233480 | tf_op jit(solution)/shard_map/ppermute | solution.py:48
  42.8 1.6 %collective-permute-start.12 = (f32[152,128]{1,0:T(8,128)S(1)}, f32[152,128]{1,0:T(8,128)S(1)}, u32[]{:S(2)}, u32[]{:S(2)}) collective-permute-start(f32[152,128]{1,0:T(8,128)S(1)} %get-tuple-element.42), channel_id=1, source_target_pairs={{0,130},{1,131},{2,0},{3,1},{4,134},{5,135},{6,4},{7,5},{8,138},{9... | collective-permute-start | bytes 233480 | tf_op jit(solution)/shard_map/ppermute | solution.py:48
  44.4 1.9 %collective-permute-start.11 = (f32[128,128]{1,0:T(8,128)S(1)}, f32[128,128]{1,0:T(8,128)S(1)}, u32[]{:S(2)}, u32[]{:S(2)}) collective-permute-start(f32[128,128]{1,0:T(8,128)S(1)} %get-tuple-element.41), channel_id=1, source_target_pairs={{0,32},{1,33},{2,34},{3,35},{4,36},{5,37},{6,38},{7,39},{8,40},{9,... | collective-permute-start | bytes 196616 | tf_op jit(solution)/shard_map/ppermute | solution.py:48
  46.3 0.0 collective-permute-done.9.refs_1_
  46.3 0.1 collective-permute-start.13
  46.4 2.2 %collective-permute-done.11.refs_3_ = f32[128,128]{1,0:T(8,128)S(1)} collective-permute-done((f32[128,128]{1,0:T(8,128)S(1)}, f32[128,128]{1,0:T(8,128)S(1)}, u32[]{:S(2)}, u32[]{:S(2)}) %collective-permute-start.11) | collective-permute-done | bytes 65568 | tf_op jit(solution)/shard_map/ppermute | solution.py:48
  48.6 3.1 %collective-permute-done.13.refs_5_ = f32[128,128]{1,0:T(8,128)S(1)} collective-permute-done((f32[128,128]{1,0:T(8,128)S(1)}, f32[128,128]{1,0:T(8,128)S(1)}, u32[]{:S(2)}, u32[]{:S(2)}) %collective-permute-start.13) | collective-permute-done | bytes 65568 | tf_op jit(solution)/shard_map/ppermute | solution.py:48
  51.8 0.0 collective-permute-done.8.refs_0_
  51.8 0.0 collective-permute-done.10.refs_2_
  51.8 0.0 collective-permute-done.12.refs_4_
  51.8 0.1 shard_map.124
  51.8 18.4 %all_to_all.5.got = f32[8,56,128]{2,1,0:T(8,128)S(1)} all-to-all(f32[8,56,128]{2,1,0:T(8,128)S(1)} %shard_map.124), channel_id=1, replica_groups=mesh['gx'=8,'gy'=8,'gz'=4] {'gy'}, dimensions={0} | all-to-all | bytes 458752 | tf_op jit(solution)/shard_map/all_to_all | solution.py:404
  70.2 0.0 copy-done
  70.2 0.0 copy-done.1
  70.2 0.0 copy-done.2
  70.2 0.7 shard_map.125
Async XLA Ops:
  15.7 2.7 %collective-permute-start.2 = (f32[2048,128]{1,0:T(8,128)S(1)}, f32[2048,128]{1,0:T(8,128)S(1)}, u32[]{:S(2)}, u32[]{:S(2)}) collective-permute-start(f32[2048,128]{1,0:T(8,128)S(1)} %get-tuple-element.30), channel_id=1, source_target_pairs={{0,1},{1,0},{2,3},{3,2},{4,5},{5,4},{6,7},{7,6},{8,9},{9,8},{10,11... | collective-permute-start | bytes 3145736 | tf_op jit(solution)/shard_map/ppermute | solution.py:48
  15.8 6.1 %collective-permute-start = (f32[2072,128]{1,0:T(8,128)S(1)}, f32[2072,128]{1,0:T(8,128)S(1)}, u32[]{:S(2)}, u32[]{:S(2)}) collective-permute-start(f32[2072,128]{1,0:T(8,128)S(1)} %get-tuple-element.27), channel_id=1, source_target_pairs={{0,1},{1,0},{2,3},{3,2},{4,5},{5,4},{6,7},{7,6},{8,9},{9,8},{10,11... | collective-permute-start | bytes 3182600 | tf_op jit(solution)/shard_map/ppermute | solution.py:48
  18.6 10.2 %collective-permute-start.3 = (f32[512,128]{1,0:T(8,128)S(1)}, f32[512,128]{1,0:T(8,128)S(1)}, u32[]{:S(2)}, u32[]{:S(2)}) collective-permute-start(f32[512,128]{1,0:T(8,128)S(1)} %get-tuple-element.31), channel_id=1, source_target_pairs={{0,128},{1,129},{2,130},{3,131},{4,132},{5,133},{6,134},{7,135},{8... | collective-permute-start | bytes 786440 | tf_op jit(solution)/shard_map/ppermute | solution.py:48
  22.0 14.5 %collective-permute-start.1 = (f32[536,128]{1,0:T(8,128)S(1)}, f32[536,128]{1,0:T(8,128)S(1)}, u32[]{:S(2)}, u32[]{:S(2)}) collective-permute-start(f32[536,128]{1,0:T(8,128)S(1)} %get-tuple-element.28), channel_id=1, source_target_pairs={{0,64},{1,65},{2,66},{3,67},{4,68},{5,69},{6,70},{7,71},{8,72},{9,... | collective-permute-start | bytes 823304 | tf_op jit(solution)/shard_map/ppermute | solution.py:48
  23.5 13.0 %collective-permute-start.4 = (f32[536,128]{1,0:T(8,128)S(1)}, f32[536,128]{1,0:T(8,128)S(1)}, u32[]{:S(2)}, u32[]{:S(2)}) collective-permute-start(f32[536,128]{1,0:T(8,128)S(1)} %get-tuple-element.32), channel_id=1, source_target_pairs={{0,32},{1,33},{2,34},{3,35},{4,36},{5,37},{6,38},{7,39},{8,40},{9,... | collective-permute-start | bytes 823304 | tf_op jit(solution)/shard_map/ppermute | solution.py:48
  25.6 12.2 %collective-permute-start.6 = (f32[536,128]{1,0:T(8,128)S(1)}, f32[536,128]{1,0:T(8,128)S(1)}, u32[]{:S(2)}, u32[]{:S(2)}) collective-permute-start(f32[536,128]{1,0:T(8,128)S(1)} %get-tuple-element.34), channel_id=1, source_target_pairs={{0,96},{1,97},{2,98},{3,99},{4,100},{5,101},{6,102},{7,103},{8,104... | collective-permute-start | bytes 823304 | tf_op jit(solution)/shard_map/ppermute | solution.py:48
  25.6 8.7 %collective-permute-start.5 = (f32[512,128]{1,0:T(8,128)S(1)}, f32[512,128]{1,0:T(8,128)S(1)}, u32[]{:S(2)}, u32[]{:S(2)}) collective-permute-start(f32[512,128]{1,0:T(8,128)S(1)} %get-tuple-element.33), channel_id=1, source_target_pairs={{0,2},{1,3},{2,128},{3,129},{4,6},{5,7},{6,132},{7,133},{8,10},{9,... | collective-permute-start | bytes 786440 | tf_op jit(solution)/shard_map/ppermute | solution.py:48
  28.8 7.8 %collective-permute-start.7 = (f32[512,128]{1,0:T(8,128)S(1)}, f32[512,128]{1,0:T(8,128)S(1)}, u32[]{:S(2)}, u32[]{:S(2)}) collective-permute-start(f32[512,128]{1,0:T(8,128)S(1)} %get-tuple-element.35), channel_id=1, source_target_pairs={{0,130},{1,131},{2,0},{3,1},{4,134},{5,135},{6,4},{7,5},{8,138},{9... | collective-permute-start | bytes 786440 | tf_op jit(solution)/shard_map/ppermute | solution.py:48
  38.0 32.3 %copy-start = (f32[169,16]{0,1:T(8,128)S(1)}, f32[169,16]{0,1:T(8,128)}, u32[]{:S(2)}) copy-start(f32[169,16]{0,1:T(8,128)} %param.19) | copy-start | bytes 32452
  38.0 32.3 %copy-start.1 = (f32[3072]{0:T(1024)S(1)}, f32[3072]{0:T(1024)}, u32[]{:S(2)}) copy-start(f32[3072]{0:T(1024)} %param.17) | copy-start | bytes 36868
  38.0 32.2 %copy-start.2 = (f32[1024]{0:T(1024)S(1)}, f32[1024]{0:T(1024)}, u32[]{:S(2)}) copy-start(f32[1024]{0:T(1024)} %param.18) | copy-start | bytes 12292
  38.0 8.3 %collective-permute-start.9 = (f32[128,128]{1,0:T(8,128)S(1)}, f32[128,128]{1,0:T(8,128)S(1)}, u32[]{:S(2)}, u32[]{:S(2)}) collective-permute-start(f32[128,128]{1,0:T(8,128)S(1)} %get-tuple-element.39), channel_id=1, source_target_pairs={{0,64},{1,65},{2,66},{3,67},{4,68},{5,69},{6,70},{7,71},{8,72},{9,... | collective-permute-start | bytes 196616 | tf_op jit(solution)/shard_map/ppermute | solution.py:48
  39.6 12.2 %collective-permute-start.8 = (f32[152,128]{1,0:T(8,128)S(1)}, f32[152,128]{1,0:T(8,128)S(1)}, u32[]{:S(2)}, u32[]{:S(2)}) collective-permute-start(f32[152,128]{1,0:T(8,128)S(1)} %get-tuple-element.38), channel_id=1, source_target_pairs={{0,128},{1,129},{2,130},{3,131},{4,132},{5,133},{6,134},{7,135},{8... | collective-permute-start | bytes 233480 | tf_op jit(solution)/shard_map/ppermute | solution.py:48
  41.1 10.6 %collective-permute-start.10 = (f32[152,128]{1,0:T(8,128)S(1)}, f32[152,128]{1,0:T(8,128)S(1)}, u32[]{:S(2)}, u32[]{:S(2)}) collective-permute-start(f32[152,128]{1,0:T(8,128)S(1)} %get-tuple-element.40), channel_id=1, source_target_pairs={{0,2},{1,3},{2,128},{3,129},{4,6},{5,7},{6,132},{7,133},{8,10},{9,... | collective-permute-start | bytes 233480 | tf_op jit(solution)/shard_map/ppermute | solution.py:48
  42.8 9.0 %collective-permute-start.12 = (f32[152,128]{1,0:T(8,128)S(1)}, f32[152,128]{1,0:T(8,128)S(1)}, u32[]{:S(2)}, u32[]{:S(2)}) collective-permute-start(f32[152,128]{1,0:T(8,128)S(1)} %get-tuple-element.42), channel_id=1, source_target_pairs={{0,130},{1,131},{2,0},{3,1},{4,134},{5,135},{6,4},{7,5},{8,138},{9... | collective-permute-start | bytes 233480 | tf_op jit(solution)/shard_map/ppermute | solution.py:48
  44.4 4.3 %collective-permute-start.11 = (f32[128,128]{1,0:T(8,128)S(1)}, f32[128,128]{1,0:T(8,128)S(1)}, u32[]{:S(2)}, u32[]{:S(2)}) collective-permute-start(f32[128,128]{1,0:T(8,128)S(1)} %get-tuple-element.41), channel_id=1, source_target_pairs={{0,32},{1,33},{2,34},{3,35},{4,36},{5,37},{6,38},{7,39},{8,40},{9,... | collective-permute-start | bytes 196616 | tf_op jit(solution)/shard_map/ppermute | solution.py:48
  46.3 5.5 %collective-permute-start.13 = (f32[128,128]{1,0:T(8,128)S(1)}, f32[128,128]{1,0:T(8,128)S(1)}, u32[]{:S(2)}, u32[]{:S(2)}) collective-permute-start(f32[128,128]{1,0:T(8,128)S(1)} %get-tuple-element.43), channel_id=1, source_target_pairs={{0,96},{1,97},{2,98},{3,99},{4,100},{5,101},{6,102},{7,103},{8,104... | collective-permute-start | bytes 196616 | tf_op jit(solution)/shard_map/ppermute | solution.py:48
